TPU v7x, 256 devices: a whole 4x4x8 slice. The times are simulated.
256 devices in a mesh: slab: 32 (over x, y, core), probe: 8 (over z).
Axes of the slice: x: 4, y: 4, z: 8, core: 2. Of those that a mesh axis runs over, the one named last changes fastest.
Arguments:
- probes: float32 [16, 3, 64, 128, 128], P('probe', None, 'slab'), may hold values from -50 to 50
- earlier: float32 [16, 3, 64, 128, 128], P(None, None, 'slab', 'probe'), may hold values from -16 to 16
- modulus: float32 [64, 128, 128], P('slab'), may hold values from 0.5 to 2
- tangent: float32 [6, 64, 128, 128], P(None, 'slab'), may hold values from -0.3 to 2, as said below
Outputs:
- basis: float32 [16, 3, 64, 128, 128], P('probe', None, 'slab')
- correlation: float32 [16, 16], replicated
Inputs may be any that keep to these rules, and one draw needn't show every extreme that they name: `tangent`: entries 0 to 2 lie in 1 to 2, entries 3 to 5 in -0.3 to 0.3.
All inputs are finite; a program needn't handle non-finite values.
Results may differ from a plain program's by a relative error of at most 0.00014.
Values sent between devices are 32-bit elements; how exact they have to be, the bound alone decides.
No kernel may reach another device: no remote copies, remote signals or barrier semaphores. Data moves between devices by JAX's collectives and lax.ppermute only.
A program may use at most 64 MiB of HBM per device.

v0:
```python
import jax
import jax.numpy as jnp
from jax import lax
from jax.sharding import PartitionSpec as P


def padded_2(cells, sides, width):
    for axis, dim in sides:
        count = lax.axis_size(axis)
        ends = count - 1
        head = lax.slice_in_dim(cells, 0, width, axis=dim)
        tail = lax.slice_in_dim(cells, cells.shape[dim] - width, cells.shape[dim], axis=dim)
        cells = jnp.concatenate(
            [
                lax.ppermute(tail, axis, [(i, (i + 1) % count) for i in range(ends)]),
                cells,
                lax.ppermute(head, axis, [((i + 1) % count, i) for i in range(ends)]),
            ],
            axis=dim,
        )
    return cells


def scaled_tangent(vectors, modulus, tensor):
    planes = vectors.shape[2] - 2
    height = vectors.shape[3]
    breadth = vectors.shape[4]
    padded = jnp.pad(vectors, ((0, 0), (0, 0), (0, 0), (1, 1), (1, 1)))
    mod_pad = jnp.pad(modulus, ((0, 0), (1, 1), (1, 1)))
    centre = padded[:, :, 1 : planes + 1, 1 : height + 1, 1 : breadth + 1]
    mod_centre = mod_pad[1 : planes + 1, 1 : height + 1, 1 : breadth + 1]
    summed = jnp.zeros_like(centre)
    for step_z in (-1, 0, 1):
        for step_y in (-1, 0, 1):
            for step_x in (-1, 0, 1):
                reach = abs(step_z) + abs(step_y) + abs(step_x)
                if reach == 0:
                    continue
                weight = (0.3, 0.1, 0.05)[reach - 1]
                nearby = padded[
                    :,
                    :,
                    1 + step_z : planes + 1 + step_z,
                    1 + step_y : height + 1 + step_y,
                    1 + step_x : breadth + 1 + step_x,
                ]
                mod_near = mod_pad[
                    1 + step_z : planes + 1 + step_z,
                    1 + step_y : height + 1 + step_y,
                    1 + step_x : breadth + 1 + step_x,
                ]
                edge_coef = 0.5 * weight * (mod_centre + mod_near)
                summed = summed + edge_coef * (centre - nearby)
    first_c = centre[:, 0]
    second_c = centre[:, 1]
    third_c = centre[:, 2]
    local_part = jnp.stack(
        [
            tensor[0] * first_c + tensor[3] * second_c + tensor[4] * third_c,
            tensor[3] * first_c + tensor[1] * second_c + tensor[5] * third_c,
            tensor[4] * first_c + tensor[5] * second_c + tensor[2] * third_c,
        ],
        axis=1,
    )
    return (summed + local_part - 8.0 * centre) / 8.0


def body(probes, earlier, modulus, tangent):
    depth = probes.shape[2]
    slabs = lax.axis_size("slab")
    highest = lax.Precision.HIGHEST
    ext_probe, ext_mod = (
        padded_2(probes, (("slab", 2),), 1),
        padded_2(modulus[None, None], (("slab", 2),), 1),
    )
    mod_wide = ext_mod[0, 0]
    first = scaled_tangent(ext_probe, mod_wide, tangent)
    ext_first = padded_2(first, (("slab", 2),), 1)
    second = scaled_tangent(ext_first, mod_wide, tangent)
    filtered = 2.0 * second - probes
    rows_y = lax.all_to_all(filtered, "probe", split_axis=3, concat_axis=0, tiled=True)
    flat_y = rows_y.reshape(rows_y.shape[0], -1)
    flat_q = earlier.reshape(earlier.shape[0], -1)
    scale = jnp.sqrt(jnp.float32(3 * depth * slabs * probes.shape[3] * probes.shape[4]))
    qq_part = jnp.dot(flat_q, flat_q.T, precision=highest)
    qy_part = jnp.dot(flat_q, flat_y.T, precision=highest)
    gram_earlier, cross = lax.psum((qq_part, qy_part), ("slab", "probe"))
    coeff = jax.scipy.linalg.cho_solve((jnp.linalg.cholesky(gram_earlier), True), cross)
    residue = flat_y - jnp.dot(coeff.T, flat_q, precision=highest)
    group_width = probes.shape[0]
    groups_total = lax.axis_size("probe")
    groups = [residue[k * group_width : (k + 1) * group_width] for k in range(groups_total)]
    for k in range(groups_total):
        own_group = groups[k]
        group_gram = lax.psum(jnp.dot(own_group, own_group.T, precision=highest), ("slab", "probe"))
        own_group = jax.scipy.linalg.solve_triangular(
            jnp.linalg.cholesky(group_gram), own_group, lower=True
        )
        later = groups[k + 1 :]
        if len(later) > 0:
            remaining = jnp.concatenate(later, axis=0)
            along = lax.psum(jnp.dot(remaining, own_group.T, precision=highest), ("slab", "probe"))
            remaining = remaining - jnp.dot(along, own_group, precision=highest)
            later = [remaining[m * group_width : (m + 1) * group_width] for m in range(len(later))]
        groups = groups[:k] + [own_group] + later
    basis_rows = jnp.concatenate(groups, axis=0)
    basis_rows = (basis_rows * scale).reshape(rows_y.shape)
    basis = lax.all_to_all(basis_rows, "probe", split_axis=0, concat_axis=3, tiled=True)
    return (basis, coeff * scale)


def solution(mesh):
    in_specs = (
        P("probe", None, "slab", None, None),
        P(None, None, "slab", "probe", None),
        P("slab", None, None),
        P(None, "slab", None, None),
    )
    out_specs = (P("probe", None, "slab", None, None), P())
    return jax.shard_map(body, mesh=mesh, in_specs=in_specs, out_specs=out_specs, check_vma=False)
```

profile of v0, /device:TPU:2, one launch (start us, length us, event | category | flops | bytes accessed | tf_op | source)
XLA Modules:
  0.0 1344.2 jit_solution(6016094942642158708)
XLA Ops:
  0.7 1.0 fusion.249
  1.6 1.9 collective-permute-start
  3.5 5.8 collective-permute-start.1
  9.3 1.2 fusion.248
  10.5 1.9 collective-permute-start.2
  12.4 5.8 collective-permute-start.3
  18.2 1.3 slice_bitcast_fusion.5
  19.5 1.1 multiply_add_fusion.5
  21.0 1.2 fusion.133
  22.3 1.2 collective-permute-done.3
  23.4 1.5 select_maximum_fusion.2
  24.9 5.1 broadcast_multiply_fusion.1
  30.3 1.9 collective-permute-start.4
  32.2 5.9 collective-permute-start.5
  38.1 2.2 multiply_add_fusion.2
  40.3 1.3 collective-permute-done.4
  41.7 1.8 collective-permute-done.5
  43.4 1.5 select_maximum_fusion
  44.9 5.5 fusion.10
  50.4 1.5 copy.134
  51.9 8.5 all-to-all-start
  60.4 1.4 convolution_bitcast_fusion.2
  61.8 23.6 %all-to-all-done = f32[2,3,2,128,128]{4,1,2,0,3:T(4,128)S(1)} async-done(((f32[2,3,2,128,128]{4,1,2,0,3:T(4,128)}), f32[2,3,2,128,128]{4,1,2,0,3:T(4,128)S(1)}, u32[]{:S(2)}, u32[]{:S(2)}) %all-to-all-start) | async-done | bytes 786464 | tf_op jit(solution)/shard_map/all_to_all | solution.py:81
  85.9 1.4 convolution_bitcast_fusion.1
  87.2 76.8 %all-reduce.3 = (f32[16,16]{0,1:T(8,128)S(1)}, f32[16,16]{0,1:T(8,128)S(1)}) all-reduce(f32[16,16]{0,1:T(8,128)S(1)} %convolution_bitcast_fusion.1, f32[16,16]{0,1:T(8,128)S(1)} %convolution_bitcast_fusion.2), channel_id=1, replica_groups=mesh['slab'=32,'probe'=8] {'slab','probe'}, use_global_device_ids=true, to_apply=%region_3.4 | all-reduce | flops 512 | bytes 4096 | tf_op jit(solution)/shard_map/psum | solution.py:87
  164.1 1.5 cholesky.30
  166.9 1.2 custom-call.15
  168.3 0.8 broadcast_multiply_fusion.2
  169.1 1.2 convolution_subtract_fusion
  170.2 0.9 fusion.214
  171.2 74.2 %psum.121 = f32[2,2]{0,1:T(2,128)S(1)} all-reduce(f32[2,2]{0,1:T(2,128)S(1)} %fusion.214), channel_id=1, replica_groups=mesh['slab'=32,'probe'=8] {'slab','probe'}, use_global_device_ids=true, to_apply=%region_4.5 | all-reduce | flops 4 | bytes 32 | tf_op jit(solution)/shard_map/psum | solution.py:95
  247.8 1.0 fusion.124
  248.8 73.3 %psum.122 = f32[14,2]{0,1:T(2,128)S(1)} all-reduce(f32[14,2]{0,1:T(2,128)S(1)} %fusion.124), channel_id=1, replica_groups=mesh['slab'=32,'probe'=8] {'slab','probe'}, use_global_device_ids=true, to_apply=%region_7.10 | all-reduce | flops 28 | bytes 224 | tf_op jit(solution)/shard_map/psum | solution.py:102
  322.1 0.9 convolution_subtract_fusion.3
  323.0 0.9 fusion.210
  324.0 74.3 %psum.123 = f32[2,2]{0,1:T(2,128)S(1)} all-reduce(f32[2,2]{0,1:T(2,128)S(1)} %fusion.210), channel_id=1, replica_groups=mesh['slab'=32,'probe'=8] {'slab','probe'}, use_global_device_ids=true, to_apply=%region_8.11 | all-reduce | flops 4 | bytes 32 | tf_op jit(solution)/shard_map/psum | solution.py:95
  400.6 1.0 fusion.122
  401.6 73.3 %psum.124 = f32[12,2]{0,1:T(2,128)S(1)} all-reduce(f32[12,2]{0,1:T(2,128)S(1)} %fusion.122), channel_id=1, replica_groups=mesh['slab'=32,'probe'=8] {'slab','probe'}, use_global_device_ids=true, to_apply=%region_9.12 | all-reduce | flops 24 | bytes 192 | tf_op jit(solution)/shard_map/psum | solution.py:102
  475.0 0.9 convolution_subtract_fusion.2
  475.9 0.9 fusion.206
  476.8 74.4 %psum.125 = f32[2,2]{0,1:T(2,128)S(1)} all-reduce(f32[2,2]{0,1:T(2,128)S(1)} %fusion.206), channel_id=1, replica_groups=mesh['slab'=32,'probe'=8] {'slab','probe'}, use_global_device_ids=true, to_apply=%region_10.13 | all-reduce | flops 4 | bytes 32 | tf_op jit(solution)/shard_map/psum | solution.py:95
  553.6 1.0 fusion.120
  554.6 73.3 %psum.126 = f32[10,2]{0,1:T(2,128)S(1)} all-reduce(f32[10,2]{0,1:T(2,128)S(1)} %fusion.120), channel_id=1, replica_groups=mesh['slab'=32,'probe'=8] {'slab','probe'}, use_global_device_ids=true, to_apply=%region_11.14 | all-reduce | flops 20 | bytes 160 | tf_op jit(solution)/shard_map/psum | solution.py:102
  627.9 0.9 convolution_subtract_fusion.1
  628.8 0.9 fusion.202
  629.8 74.2 %psum.127 = f32[2,2]{0,1:T(2,128)S(1)} all-reduce(f32[2,2]{0,1:T(2,128)S(1)} %fusion.202), channel_id=1, replica_groups=mesh['slab'=32,'probe'=8] {'slab','probe'}, use_global_device_ids=true, to_apply=%region_12.15 | all-reduce | flops 4 | bytes 32 | tf_op jit(solution)/shard_map/psum | solution.py:95
  706.4 0.9 fusion.128
  707.3 73.3 %psum.128 = f32[8,2]{0,1:T(2,128)S(1)} all-reduce(f32[8,2]{0,1:T(2,128)S(1)} %fusion.128), channel_id=1, replica_groups=mesh['slab'=32,'probe'=8] {'slab','probe'}, use_global_device_ids=true, to_apply=%region_13.16 | all-reduce | flops 16 | bytes 128 | tf_op jit(solution)/shard_map/psum | solution.py:102
  781.2 0.9 fusion.198
  782.2 74.2 %psum.129 = f32[2,2]{0,1:T(2,128)S(1)} all-reduce(f32[2,2]{0,1:T(2,128)S(1)} %fusion.198), channel_id=1, replica_groups=mesh['slab'=32,'probe'=8] {'slab','probe'}, use_global_device_ids=true, to_apply=%region_14.17 | all-reduce | flops 4 | bytes 32 | tf_op jit(solution)/shard_map/psum | solution.py:95
  858.8 0.9 fusion.126
  859.7 73.3 %psum.130 = f32[6,2]{0,1:T(2,128)S(1)} all-reduce(f32[6,2]{0,1:T(2,128)S(1)} %fusion.126), channel_id=1, replica_groups=mesh['slab'=32,'probe'=8] {'slab','probe'}, use_global_device_ids=true, to_apply=%region_15.18 | all-reduce | flops 12 | bytes 96 | tf_op jit(solution)/shard_map/psum | solution.py:102
  933.6 0.9 fusion.194
  934.5 74.4 %psum.131 = f32[2,2]{0,1:T(2,128)S(1)} all-reduce(f32[2,2]{0,1:T(2,128)S(1)} %fusion.194), channel_id=1, replica_groups=mesh['slab'=32,'probe'=8] {'slab','probe'}, use_global_device_ids=true, to_apply=%region_16.19 | all-reduce | flops 4 | bytes 32 | tf_op jit(solution)/shard_map/psum | solution.py:95
  1011.4 0.9 fusion.130
  1012.3 73.3 %psum.132 = f32[4,2]{0,1:T(2,128)S(1)} all-reduce(f32[4,2]{0,1:T(2,128)S(1)} %fusion.130), channel_id=1, replica_groups=mesh['slab'=32,'probe'=8] {'slab','probe'}, use_global_device_ids=true, to_apply=%region_17.20 | all-reduce | flops 8 | bytes 64 | tf_op jit(solution)/shard_map/psum | solution.py:102
  1086.2 0.9 fusion.190
  1087.1 74.2 %psum.133 = f32[2,2]{0,1:T(2,128)S(1)} all-reduce(f32[2,2]{0,1:T(2,128)S(1)} %fusion.190), channel_id=1, replica_groups=mesh['slab'=32,'probe'=8] {'slab','probe'}, use_global_device_ids=true, to_apply=%region_18.21 | all-reduce | flops 4 | bytes 32 | tf_op jit(solution)/shard_map/psum | solution.py:95
  1163.7 0.9 fusion.186
  1164.7 73.3 %psum.134 = f32[2,2]{1,0:T(2,128)S(1)} all-reduce(f32[2,2]{1,0:T(2,128)S(1)} %fusion.186), channel_id=1, replica_groups=mesh['slab'=32,'probe'=8] {'slab','probe'}, use_global_device_ids=true, to_apply=%region_19.22 | all-reduce | flops 4 | bytes 32 | tf_op jit(solution)/shard_map/psum | solution.py:102
  1238.5 0.9 fusion.250
  1239.4 74.2 %psum.135 = f32[2,2]{0,1:T(2,128)S(1)} all-reduce(f32[2,2]{0,1:T(2,128)S(1)} %fusion.250), channel_id=1, replica_groups=mesh['slab'=32,'probe'=8] {'slab','probe'}, use_global_device_ids=true, to_apply=%region_20.23 | all-reduce | flops 4 | bytes 32 | tf_op jit(solution)/shard_map/psum | solution.py:95
  1316.4 26.6 %all_to_all.33 = f32[16,3,2,16,128]{4,3,2,1,0:T(8,128)S(1)} all-to-all(f32[16,3,2,16,128]{4,3,2,1,0:T(8,128)S(1)} %broadcast_multiply_fusion), channel_id=1, replica_groups=mesh['slab'=32,'probe'=8] {'probe'}, dimensions={0} | all-to-all | bytes 1572864 | tf_op jit(solution)/shard_map/all_to_all | solution.py:108
  1343.0 0.9 copy.164
  (153 shorter events, 23.7 us)
Async XLA Ops:
  0.6 20.0 %copy-start.2 = (f32[2,128,128]{2,1,0:T(8,128)S(1)}, f32[2,128,128]{2,1,0:T(8,128)}, u32[]{:S(2)}) copy-start(f32[2,128,128]{2,1,0:T(8,128)} %param.9) | copy-start | bytes 393220
  0.6 18.9 %copy-start = (f32[2,3,2,128,128]{4,3,2,1,0:T(8,128)S(1)}, f32[2,3,2,128,128]{4,3,2,1,0:T(8,128)}, u32[]{:S(2)}) copy-start(f32[2,3,2,128,128]{4,3,2,1,0:T(8,128)} %param.7) | copy-start | bytes 2359300
  1.6 19.0 %collective-permute-start = (f32[1,1,1,128,128]{4,3,2,1,0:T(8,128)S(1)}, f32[1,1,1,128,128]{4,3,2,1,0:T(8,128)S(1)}, u32[]{:S(2)}, u32[]{:S(2)}) collective-permute-start(f32[1,1,1,128,128]{4,3,2,1,0:T(8,128)S(1)} %get-tuple-element.52), channel_id=1, source_target_pairs={{0,8},{8,16},{16,24},{24,32},{32,40},{40,48},{48,56},{56,64},{64,7... | collective-permute-start | bytes 196616 | tf_op jit(solution)/shard_map/ppermute | solution.py:15
  3.5 17.1 %collective-permute-start.1 = (f32[1,1,1,128,128]{4,3,2,1,0:T(8,128)S(1)}, f32[1,1,1,128,128]{4,3,2,1,0:T(8,128)S(1)}, u32[]{:S(2)}, u32[]{:S(2)}) collective-permute-start(f32[1,1,1,128,128]{4,3,2,1,0:T(8,128)S(1)} %get-tuple-element.53), channel_id=1, source_target_pairs={{8,0},{16,8},{24,16},{32,24},{40,32},{48,40},{56,48},{64,56},{72,6... | collective-permute-start | bytes 196616 | tf_op jit(solution)/shard_map/ppermute | solution.py:17
  10.5 11.8 collective-permute-start.2
  12.4 11.0 collective-permute-start.3
  19.4 1.2 copy-start.21
  19.4 1.2 copy-start.22
  19.5 1.2 copy-start.23
  19.5 1.2 copy-start.24
  19.5 1.2 copy-start.25
  19.5 1.2 copy-start.26
  21.0 9.1 copy-start.3
  22.1 7.9 copy-start.4
  22.1 7.9 copy-start.5
  22.1 7.9 copy-start.6
  22.1 7.9 copy-start.7
  22.1 7.9 copy-start.8
  22.1 7.9 copy-start.9
  22.2 7.9 copy-start.10
  22.2 7.9 copy-start.11
  22.2 7.9 copy-start.12
  22.2 7.9 copy-start.13
  22.2 7.9 copy-start.14
  22.2 7.9 copy-start.15
  22.2 7.9 copy-start.16
  22.2 7.9 copy-start.17
  22.2 7.9 copy-start.18
  22.2 7.9 copy-start.19
  22.3 7.9 copy-start.20
  30.3 11.4 collective-permute-start.4
  32.2 11.2 collective-permute-start.5
  50.4 10.0 copy-start.1
  51.9 33.5 %all-to-all-start = ((f32[2,3,2,128,128]{4,1,2,0,3:T(4,128)}), f32[2,3,2,128,128]{4,1,2,0,3:T(4,128)S(1)}, u32[]{:S(2)}, u32[]{:S(2)}) async-start(f32[2,3,2,128,128]{4,1,2,0,3:T(4,128)} %copy.134), calls=%async_computation | async-start | bytes 2097152 | tf_op jit(solution)/shard_map/all_to_all | solution.py:81
where the time goes:
time: 1360 us; the launch traced here: 1340 us
  blocking collectives  1210 us (89%)
  other arithmetic  36 us (3%)
  starting transfers between devices  31.7 us (2%)
  matrix products  28.7 us (2%)
  waiting for transfers between devices  27.9 us (2%)
    psum x8, blocking collectives, body(): lax.psum(jnp.dot(own_group, own_group.T, precision=highest), ('slab', 'pr...  594 us
    psum x7, blocking collectives, body(): lax.psum(jnp.dot(remaining, own_group.T, precision=highest), ('slab', 'pr...  513 us
    psum x1, blocking collectives, body(): gram_earlier, cross = lax.psum((qq_part, qy_part), ('slab', 'probe'))  76.8 us
  transfers between devices with their start and end apart: 7, of which 4 were waited for; matrix products, arithmetic and copies ran while one was open for 1% of the time, Pallas kernels for 0%

commit v1 on v0

--- a/solution.py
+++ b/solution.py
@@ -65,6 +65,12 @@
     return (summed + local_part - 8.0 * centre) / 8.0
 
 
+def sum_over(block, axis):
+    count = lax.axis_size(axis)
+    copies = jnp.broadcast_to(block[None], (count,) + block.shape)
+    return jnp.sum(lax.all_to_all(copies, axis, 0, 0, tiled=True), axis=0)
+
+
 def body(probes, earlier, modulus, tangent):
     depth = probes.shape[2]
     slabs = lax.axis_size("slab")
@@ -79,32 +85,20 @@
     second = scaled_tangent(ext_first, mod_wide, tangent)
     filtered = 2.0 * second - probes
     rows_y = lax.all_to_all(filtered, "probe", split_axis=3, concat_axis=0, tiled=True)
-    flat_y = rows_y.reshape(rows_y.shape[0], -1)
-    flat_q = earlier.reshape(earlier.shape[0], -1)
+    kept = earlier.shape[0]
+    both = jnp.concatenate([earlier, rows_y], axis=0)
     scale = jnp.sqrt(jnp.float32(3 * depth * slabs * probes.shape[3] * probes.shape[4]))
-    qq_part = jnp.dot(flat_q, flat_q.T, precision=highest)
-    qy_part = jnp.dot(flat_q, flat_y.T, precision=highest)
-    gram_earlier, cross = lax.psum((qq_part, qy_part), ("slab", "probe"))
-    coeff = jax.scipy.linalg.cho_solve((jnp.linalg.cholesky(gram_earlier), True), cross)
-    residue = flat_y - jnp.dot(coeff.T, flat_q, precision=highest)
-    group_width = probes.shape[0]
-    groups_total = lax.axis_size("probe")
-    groups = [residue[k * group_width : (k + 1) * group_width] for k in range(groups_total)]
-    for k in range(groups_total):
-        own_group = groups[k]
-        group_gram = lax.psum(jnp.dot(own_group, own_group.T, precision=highest), ("slab", "probe"))
-        own_group = jax.scipy.linalg.solve_triangular(
-            jnp.linalg.cholesky(group_gram), own_group, lower=True
-        )
-        later = groups[k + 1 :]
-        if len(later) > 0:
-            remaining = jnp.concatenate(later, axis=0)
-            along = lax.psum(jnp.dot(remaining, own_group.T, precision=highest), ("slab", "probe"))
-            remaining = remaining - jnp.dot(along, own_group, precision=highest)
-            later = [remaining[m * group_width : (m + 1) * group_width] for m in range(len(later))]
-        groups = groups[:k] + [own_group] + later
-    basis_rows = jnp.concatenate(groups, axis=0)
-    basis_rows = (basis_rows * scale).reshape(rows_y.shape)
+    dims = (1, 2, 3, 4)
+    gram = lax.dot_general(both, both, ((dims, dims), ((), ())), precision=highest)
+    total = gram.shape[0]
+    gram = gram.reshape(8, total * total // 8)
+    gram = sum_over(sum_over(gram, "slab"), "probe").reshape(total, total)
+    factor = jnp.linalg.cholesky(gram)
+    inverse = jax.scipy.linalg.solve_triangular(factor, jnp.eye(total, dtype=jnp.float32), lower=True)
+    coeff = jnp.dot(inverse[:kept, :kept].T, factor[kept:, :kept].T, precision=highest)
+    basis_rows = lax.dot_general(
+        inverse[kept:] * scale, both, (((1,), (0,)), ((), ())), precision=highest
+    )
     basis = lax.all_to_all(basis_rows, "probe", split_axis=0, concat_axis=3, tiled=True)
     return (basis, coeff * scale)
 

time: 1360 us -> 152 us (0.11)
  blocking collectives: 1210 us -> 25.9 us
  matrix products: 28.7 us -> 3.26 us
  waiting for transfers between devices: 27.9 us -> 50.5 us
    psum x16 -> x0, blocking collectives: 1180 us -> none  [the longest x8 594 us: body(): lax.psum(jnp.dot(own_group, own_group.T, precision=highest), ('slab', 'pr...]
    all_to_all x0 -> x1, waiting for transfers between devices: none -> 21.6 us  [body(): lax.all_to_all(basis_rows, 'probe', split_axis=0, concat_axis=3, tiled=True)]
    dot_general x25 -> x3, matrix products: 23.2 us -> 3.04 us  [the longest x1 1.36 us: body(): lax.dot_general(both, both, ((dims, dims), ((), ())), precision=highest)]
  transfers between devices with their start and end apart: 7 -> 8, of which waited for: 4 -> 5; matrix products, arithmetic and copies ran while one was open for 1% -> 6% of each run, Pallas kernels for 0% -> 0%
where the time goes in v1:
time: 152 us; the launch traced here: 149 us
  waiting for transfers between devices  50.5 us (33%)
  starting transfers between devices  35.2 us (23%)
  blocking collectives  25.9 us (17%)
  other arithmetic  25 us (16%)
  local copies, waits for them, and re-layouts  8.27 us (5%)
  matrix products  3.26 us (2%)
    all_to_all x2, blocking collectives, sum_over(): return jnp.sum(lax.all_to_all(copies, axis, 0, 0, tiled=True), axis=0)  25.9 us
    all_to_all x1, waiting for transfers between devices, body(): lax.all_to_all(filtered, 'probe', split_axis=3, concat_axis=0, tiled=True)  24.6 us
    all_to_all x1, waiting for transfers between devices, body(): lax.all_to_all(basis_rows, 'probe', split_axis=0, concat_axis=3, tiled=True)  21.6 us
    ppermute x3, starting transfers between devices, padded_2(): lax.ppermute(head, axis, [((i + 1) % count, i) for i in range(ends)])  17.4 us
    all_to_all x1, starting transfers between devices, body(): lax.all_to_all(filtered, 'probe', split_axis=3, concat_axis=0, tiled=True)  8.47 us
    ppermute x3, starting transfers between devices, padded_2(): lax.ppermute(tail, axis, [(i, (i + 1) % count) for i in range(ends)])  5.76 us
    sub x1, other arithmetic, body(): filtered = 2.0 * second - probes  5.5 us
    div x1, other arithmetic, scaled_tangent(): return (summed + local_part - 8.0 * centre) / 8.0  5.17 us
  transfers between devices with their start and end apart: 8, of which 5 were waited for; matrix products, arithmetic and copies ran while one was open for 6% of the time, Pallas kernels for 0%

profile of v1, /device:TPU:2, one launch (start us, length us, event | category | flops | bytes accessed | tf_op | source)
XLA Modules:
  0.0 149.4 jit_solution(12597318986377617848)
XLA Ops:
  0.6 0.0 copy-start
  0.7 1.0 fusion.186
  1.6 1.9 %collective-permute-start = (f32[1,1,1,128,128]{4,3,2,1,0:T(8,128)S(1)}, f32[1,1,1,128,128]{4,3,2,1,0:T(8,128)S(1)}, u32[]{:S(2)}, u32[]{:S(2)}) collective-permute-start(f32[1,1,1,128,128]{4,3,2,1,0:T(8,128)S(1)} %get-tuple-element.50), channel_id=1, source_target_pairs={{0,8},{8,16},{16,24},{24,32},{32,40},{40,48},{48,56},{56,64},{64,7... | collective-permute-start | bytes 196616 | tf_op jit(solution)/shard_map/ppermute | solution.py:15
  3.5 5.8 %collective-permute-start.1 = (f32[1,1,1,128,128]{4,3,2,1,0:T(8,128)S(1)}, f32[1,1,1,128,128]{4,3,2,1,0:T(8,128)S(1)}, u32[]{:S(2)}, u32[]{:S(2)}) collective-permute-start(f32[1,1,1,128,128]{4,3,2,1,0:T(8,128)S(1)} %get-tuple-element.51), channel_id=1, source_target_pairs={{8,0},{16,8},{24,16},{32,24},{40,32},{48,40},{56,48},{64,56},{72,6... | collective-permute-start | bytes 196616 | tf_op jit(solution)/shard_map/ppermute | solution.py:17
  9.3 1.2 fusion.185
  10.5 1.9 %collective-permute-start.2 = (f32[2,3,1,128,128]{4,3,2,1,0:T(8,128)S(1)}, f32[2,3,1,128,128]{4,3,2,1,0:T(8,128)S(1)}, u32[]{:S(2)}, u32[]{:S(2)}) collective-permute-start(f32[2,3,1,128,128]{4,3,2,1,0:T(8,128)S(1)} %get-tuple-element.14), channel_id=1, source_target_pairs={{0,8},{8,16},{16,24},{24,32},{32,40},{40,48},{48,56},{56,64},{64,7... | collective-permute-start | bytes 1179656 | tf_op jit(solution)/shard_map/ppermute | solution.py:15
  12.4 5.8 %collective-permute-start.3 = (f32[2,3,1,128,128]{4,3,2,1,0:T(8,128)S(1)}, f32[2,3,1,128,128]{4,3,2,1,0:T(8,128)S(1)}, u32[]{:S(2)}, u32[]{:S(2)}) collective-permute-start(f32[2,3,1,128,128]{4,3,2,1,0:T(8,128)S(1)} %get-tuple-element.15), channel_id=1, source_target_pairs={{8,0},{16,8},{24,16},{32,24},{40,32},{48,40},{56,48},{64,56},{72,6... | collective-permute-start | bytes 1179656 | tf_op jit(solution)/shard_map/ppermute | solution.py:17
  18.2 1.3 slice_bitcast_fusion.5
  19.5 1.1 multiply_add_fusion.5
  20.6 0.0 collective-permute-done
  20.6 0.0 collective-permute-done.1
  20.7 0.2 fusion.121
  20.9 1.2 fusion.119
  22.2 0.0 collective-permute-done.2
  22.2 1.2 collective-permute-done.3
  23.4 1.5 select_maximum_fusion.2
  24.9 5.2 %broadcast_multiply_fusion = (f32[2,3,2,128,128]{4,3,2,1,0:T(8,128)S(1)}, f32[2,3,2,128,128]{4,3,2,1,0:T(8,128)S(1)}) fusion(f32[2,3,2,128,128]{4,3,2,1,0:T(8,128)S(1)} %copy-done, f32[2,1,2,128,128]{4,3,2,1,0:T(8,128)} %get-tuple-element.10, f32[2,1,2,128,128]{4,3,2,1,0:T(8,128)} %get-tuple-element.11, f32[2,1,2,128,128]{4,3,2,1,0:T(8,128)} %get-tuple-element.9, ...), kind=kLoop, calls=%fused_computation.204 | loop fusion | flops 16711680 | bytes 26214400 | tf_op jit(solution)/shard_map/div | solution.py:65
  30.1 0.0 copy-done.2
  30.1 0.0 copy-done.3
  30.1 0.0 copy-done.4
  30.1 0.0 copy-done.5
  30.1 0.0 copy-done.6
  30.1 0.0 copy-done.7
  30.2 0.0 copy-done.8
  30.2 0.0 copy-done.9
  30.2 0.0 copy-done.10
  30.2 0.0 copy-done.11
  30.2 0.0 copy-done.12
  30.2 0.0 copy-done.13
  30.2 0.0 copy-done.14
  30.2 0.0 copy-done.15
  30.2 0.0 copy-done.16
  30.2 0.0 copy-done.17
  30.3 0.1 fusion.184
  30.3 1.9 %collective-permute-start.4 = (f32[2,3,1,128,128]{4,3,2,1,0:T(8,128)S(1)}, f32[2,3,1,128,128]{4,3,2,1,0:T(8,128)S(1)}, u32[]{:S(2)}, u32[]{:S(2)}) collective-permute-start(f32[2,3,1,128,128]{4,3,2,1,0:T(8,128)S(1)} %get-tuple-element.12), channel_id=1, source_target_pairs={{0,8},{8,16},{16,24},{24,32},{32,40},{40,48},{48,56},{56,64},{64,7... | collective-permute-start | bytes 1179656 | tf_op jit(solution)/shard_map/ppermute | solution.py:15
  32.3 5.9 %collective-permute-start.5 = (f32[2,3,1,128,128]{4,3,2,1,0:T(8,128)S(1)}, f32[2,3,1,128,128]{4,3,2,1,0:T(8,128)S(1)}, u32[]{:S(2)}, u32[]{:S(2)}) collective-permute-start(f32[2,3,1,128,128]{4,3,2,1,0:T(8,128)S(1)} %get-tuple-element.13), channel_id=1, source_target_pairs={{8,0},{16,8},{24,16},{32,24},{40,32},{48,40},{56,48},{64,56},{72,6... | collective-permute-start | bytes 1179656 | tf_op jit(solution)/shard_map/ppermute | solution.py:17
  38.2 2.2 %multiply_add_fusion.2 = (f32[2,1,2,128,128]{4,3,2,1,0:T(8,128)}, f32[2,1,2,128,128]{4,3,2,1,0:T(8,128)}, f32[2,1,2,128,128]{4,3,2,1,0:T(8,128)}) fusion(f32[2,3,2,128,128]{4,3,2,1,0:T(8,128)S(1)} %get-tuple-element.4, f32[2,128,128]{2,1,0:T(8,128)} %copy-done.22, f32[2,128,128]{2,1,0:T(8,128)} %copy-done.23, f32[2,128,128]{2,1,0:T(8,128)} %copy-done.20, ...), kind=kLoop, calls=%fused_computation.208 | loop fusion | flops 983040 | bytes 2359296 | tf_op jit(solution)/shard_map/add | solution.py:59
  40.4 1.3 collective-permute-done.4
  41.7 1.8 %collective-permute-done.5 = f32[2,3,1,128,128]{4,3,2,1,0:T(8,128)S(1)} collective-permute-done((f32[2,3,1,128,128]{4,3,2,1,0:T(8,128)S(1)}, f32[2,3,1,128,128]{4,3,2,1,0:T(8,128)S(1)}, u32[]{:S(2)}, u32[]{:S(2)}) %collective-permute-start.5) | collective-permute-done | bytes 393248 | tf_op jit(solution)/shard_map/ppermute | solution.py:17
  43.5 1.5 select_maximum_fusion
  44.9 5.5 %fusion.11 = f32[2,3,2,128,128]{4,3,2,1,0:T(8,128)S(1)} fusion(f32[2,3,2,128,128]{4,3,2,1,0:T(8,128)S(1)} %copy-done, f32[2,3,2,128,128]{4,3,2,1,0:T(8,128)S(1)} %get-tuple-element.5, f32[2,3,2,128,128]{4,3,2,1,0:T(8,128)S(1)} %get-tuple-element.4, f32[2,3,4,130,130]{4,3,2,1,0:T(8,128)S(1)} %select_maximum_fusion, ...), kind=kLoop, calls=%fused_computation.46 | loop fusion | flops 16711680 | bytes 27000832 | tf_op jit(solution)/shard_map/sub | solution.py:86
  50.5 0.0 copy-start.26
  50.5 1.5 %copy.93 = f32[2,3,2,128,128]{4,1,2,0,3:T(4,128)} copy(f32[2,3,2,128,128]{4,3,2,1,0:T(8,128)S(1)} %fusion.11) | data formatting | bytes 1572864 | tf_op jit(solution)/shard_map/sub | solution.py:86
  52.0 8.5 %all-to-all-start = ((f32[2,3,2,128,128]{4,1,2,0,3:T(4,128)}), f32[2,3,2,128,128]{4,1,2,0,3:T(4,128)S(1)}, u32[]{:S(2)}, u32[]{:S(2)}) async-start(f32[2,3,2,128,128]{4,1,2,0,3:T(4,128)} %copy.93), calls=%async_computation | async-start | bytes 2097152 | tf_op jit(solution)/shard_map/all_to_all | solution.py:87
  60.5 0.5 copy.95
  60.9 24.6 %all-to-all-done = f32[2,3,2,128,128]{4,1,2,0,3:T(4,128)S(1)} async-done(((f32[2,3,2,128,128]{4,1,2,0,3:T(4,128)}), f32[2,3,2,128,128]{4,1,2,0,3:T(4,128)S(1)}, u32[]{:S(2)}, u32[]{:S(2)}) %all-to-all-start) | async-done | bytes 786464 | tf_op jit(solution)/shard_map/all_to_all | solution.py:87
  85.5 0.4 copy.94
  85.9 1.4 fusion.5
  87.3 0.1 broadcast_in_dim.10
  87.4 15.5 %all_to_all.46 = f32[32,8,128]{2,1,0:T(8,128)S(1)} all-to-all(f32[32,8,128]{2,1,0:T(8,128)S(1)} %broadcast_in_dim.11), channel_id=1, replica_groups=mesh['slab'=32,'probe'=8] {'slab'}, dimensions={0} | all-to-all | bytes 262144 | tf_op jit(solution)/shard_map/all_to_all | solution.py:71
  103.0 10.4 %all_to_all.47 = f32[8,8,128]{2,1,0:T(8,128)S(1)} all-to-all(f32[8,8,128]{2,1,0:T(8,128)S(1)} %broadcast_in_dim.12), channel_id=1, replica_groups=mesh['slab'=32,'probe'=8] {'probe'}, dimensions={0} | all-to-all | bytes 65536 | tf_op jit(solution)/shard_map/all_to_all | solution.py:71
  113.4 0.1 reshape.49
  113.4 0.1 copy.96
  113.5 2.9 %cholesky.17 = f32[32,32]{1,0:T(8,128)S(1)} custom-call(f32[32,32]{1,0:T(8,128)S(1)} %fusion.174), custom_call_target="Cholesky" | custom-call | tf_op jit(solution)/shard_map/jit(cholesky)/cholesky | solution.py:96
  116.5 0.6 compare_reduce_fusion
  117.1 0.7 select_bitcast_fusion
  117.8 2.4 %custom-call.7 = f32[1,32,32]{1,2,0:T(8,128)S(1)} custom-call(f32[1,32,32]{2,1,0:T(8,128)S(1)} %get-tuple-element.2), custom_call_target="InvertDiagBlocksLowerTriangular" | custom-call | tf_op jit(solution)/shard_map/jit(_solve_triangular)/triangular_solve | solution.py:97
  120.2 0.2 fusion.172
  120.4 0.9 fusion.3
  121.3 1.1 copy.97
  122.5 3.5 %all-to-all-start.3 = ((f32[16,3,2,16,128]{4,3,2,1,0:T(8,128)}), f32[16,3,2,16,128]{4,3,2,1,0:T(8,128)S(1)}, u32[]{:S(2)}, u32[]{:S(2)}) async-start(f32[16,3,2,16,128]{4,3,2,1,0:T(8,128)} %copy.97), calls=%async_computation.3 | async-start | bytes 1572864 | tf_op jit(solution)/shard_map/all_to_all | solution.py:102
  126.0 0.8 convolution_multiply_fusion
  126.8 21.6 %all-to-all-done.3 = f32[16,3,2,16,128]{4,3,2,1,0:T(8,128)S(1)} async-done(((f32[16,3,2,16,128]{4,3,2,1,0:T(8,128)}), f32[16,3,2,16,128]{4,3,2,1,0:T(8,128)S(1)}, u32[]{:S(2)}, u32[]{:S(2)}) %all-to-all-start.3) | async-done | bytes 786464 | tf_op jit(solution)/shard_map/all_to_all | solution.py:102
  148.4 1.0 copy.98
  (43 shorter events, 0.2 us)
Async XLA Ops:
  0.6 20.0 %copy-start.1 = (f32[2,128,128]{2,1,0:T(8,128)S(1)}, f32[2,128,128]{2,1,0:T(8,128)}, u32[]{:S(2)}) copy-start(f32[2,128,128]{2,1,0:T(8,128)} %param.6) | copy-start | bytes 393220
  0.6 18.9 %copy-start = (f32[2,3,2,128,128]{4,3,2,1,0:T(8,128)S(1)}, f32[2,3,2,128,128]{4,3,2,1,0:T(8,128)}, u32[]{:S(2)}) copy-start(f32[2,3,2,128,128]{4,3,2,1,0:T(8,128)} %param.4) | copy-start | bytes 2359300
  1.6 19.0 %collective-permute-start = (f32[1,1,1,128,128]{4,3,2,1,0:T(8,128)S(1)}, f32[1,1,1,128,128]{4,3,2,1,0:T(8,128)S(1)}, u32[]{:S(2)}, u32[]{:S(2)}) collective-permute-start(f32[1,1,1,128,128]{4,3,2,1,0:T(8,128)S(1)} %get-tuple-element.50), channel_id=1, source_target_pairs={{0,8},{8,16},{16,24},{24,32},{32,40},{40,48},{48,56},{56,64},{64,7... | collective-permute-start | bytes 196616 | tf_op jit(solution)/shard_map/ppermute | solution.py:15
  3.5 17.0 %collective-permute-start.1 = (f32[1,1,1,128,128]{4,3,2,1,0:T(8,128)S(1)}, f32[1,1,1,128,128]{4,3,2,1,0:T(8,128)S(1)}, u32[]{:S(2)}, u32[]{:S(2)}) collective-permute-start(f32[1,1,1,128,128]{4,3,2,1,0:T(8,128)S(1)} %get-tuple-element.51), channel_id=1, source_target_pairs={{8,0},{16,8},{24,16},{32,24},{40,32},{48,40},{56,48},{64,56},{72,6... | collective-permute-start | bytes 196616 | tf_op jit(solution)/shard_map/ppermute | solution.py:17
  10.5 11.7 %collective-permute-start.2 = (f32[2,3,1,128,128]{4,3,2,1,0:T(8,128)S(1)}, f32[2,3,1,128,128]{4,3,2,1,0:T(8,128)S(1)}, u32[]{:S(2)}, u32[]{:S(2)}) collective-permute-start(f32[2,3,1,128,128]{4,3,2,1,0:T(8,128)S(1)} %get-tuple-element.14), channel_id=1, source_target_pairs={{0,8},{8,16},{16,24},{24,32},{32,40},{40,48},{48,56},{56,64},{64,7... | collective-permute-start | bytes 1179656 | tf_op jit(solution)/shard_map/ppermute | solution.py:15
  12.4 11.0 %collective-permute-start.3 = (f32[2,3,1,128,128]{4,3,2,1,0:T(8,128)S(1)}, f32[2,3,1,128,128]{4,3,2,1,0:T(8,128)S(1)}, u32[]{:S(2)}, u32[]{:S(2)}) collective-permute-start(f32[2,3,1,128,128]{4,3,2,1,0:T(8,128)S(1)} %get-tuple-element.15), channel_id=1, source_target_pairs={{8,0},{16,8},{24,16},{32,24},{40,32},{48,40},{56,48},{64,56},{72,6... | collective-permute-start | bytes 1179656 | tf_op jit(solution)/shard_map/ppermute | solution.py:17
  19.4 1.2 copy-start.20
  19.4 1.2 copy-start.21
  19.5 1.2 copy-start.22
  19.5 1.2 copy-start.23
  19.5 1.2 copy-start.24
  19.5 1.2 copy-start.25
  20.9 9.2 %copy-start.2 = (f32[2,128,128]{2,1,0:T(8,128)}, f32[2,128,128]{2,1,0:T(8,128)S(1)}, u32[]{:S(2)}) copy-start(f32[2,128,128]{2,1,0:T(8,128)S(1)} %get-tuple-element.49) | copy-start | bytes 393220
  22.1 8.0 %copy-start.3 = (f32[2,128,128]{2,1,0:T(8,128)}, f32[2,128,128]{2,1,0:T(8,128)S(1)}, u32[]{:S(2)}) copy-start(f32[2,128,128]{2,1,0:T(8,128)S(1)} %get-tuple-element.22) | copy-start | bytes 393220
  22.1 8.0 %copy-start.4 = (f32[2,128,128]{2,1,0:T(8,128)}, f32[2,128,128]{2,1,0:T(8,128)S(1)}, u32[]{:S(2)}) copy-start(f32[2,128,128]{2,1,0:T(8,128)S(1)} %get-tuple-element.23) | copy-start | bytes 393220
  22.1 8.1 %copy-start.5 = (f32[2,128,128]{2,1,0:T(8,128)}, f32[2,128,128]{2,1,0:T(8,128)S(1)}, u32[]{:S(2)}) copy-start(f32[2,128,128]{2,1,0:T(8,128)S(1)} %get-tuple-element.24) | copy-start | bytes 393220
  22.1 8.1 %copy-start.6 = (f32[2,128,128]{2,1,0:T(8,128)}, f32[2,128,128]{2,1,0:T(8,128)S(1)}, u32[]{:S(2)}) copy-start(f32[2,128,128]{2,1,0:T(8,128)S(1)} %get-tuple-element.25) | copy-start | bytes 393220
  22.1 8.1 %copy-start.7 = (f32[2,128,128]{2,1,0:T(8,128)}, f32[2,128,128]{2,1,0:T(8,128)S(1)}, u32[]{:S(2)}) copy-start(f32[2,128,128]{2,1,0:T(8,128)S(1)} %get-tuple-element.26) | copy-start | bytes 393220
  22.1 8.1 %copy-start.8 = (f32[2,128,128]{2,1,0:T(8,128)}, f32[2,128,128]{2,1,0:T(8,128)S(1)}, u32[]{:S(2)}) copy-start(f32[2,128,128]{2,1,0:T(8,128)S(1)} %get-tuple-element.27) | copy-start | bytes 393220
  22.1 8.1 %copy-start.9 = (f32[2,128,128]{2,1,0:T(8,128)}, f32[2,128,128]{2,1,0:T(8,128)S(1)}, u32[]{:S(2)}) copy-start(f32[2,128,128]{2,1,0:T(8,128)S(1)} %get-tuple-element.28) | copy-start | bytes 393220
  22.1 8.1 %copy-start.10 = (f32[2,128,128]{2,1,0:T(8,128)}, f32[2,128,128]{2,1,0:T(8,128)S(1)}, u32[]{:S(2)}) copy-start(f32[2,128,128]{2,1,0:T(8,128)S(1)} %get-tuple-element.29) | copy-start | bytes 393220
  22.1 8.1 %copy-start.11 = (f32[2,128,128]{2,1,0:T(8,128)}, f32[2,128,128]{2,1,0:T(8,128)S(1)}, u32[]{:S(2)}) copy-start(f32[2,128,128]{2,1,0:T(8,128)S(1)} %get-tuple-element.30) | copy-start | bytes 393220
  22.1 8.1 %copy-start.12 = (f32[2,128,128]{2,1,0:T(8,128)}, f32[2,128,128]{2,1,0:T(8,128)S(1)}, u32[]{:S(2)}) copy-start(f32[2,128,128]{2,1,0:T(8,128)S(1)} %get-tuple-element.31) | copy-start | bytes 393220
  22.1 8.1 %copy-start.13 = (f32[2,128,128]{2,1,0:T(8,128)}, f32[2,128,128]{2,1,0:T(8,128)S(1)}, u32[]{:S(2)}) copy-start(f32[2,128,128]{2,1,0:T(8,128)S(1)} %get-tuple-element.32) | copy-start | bytes 393220
  22.2 8.1 %copy-start.14 = (f32[2,128,128]{2,1,0:T(8,128)}, f32[2,128,128]{2,1,0:T(8,128)S(1)}, u32[]{:S(2)}) copy-start(f32[2,128,128]{2,1,0:T(8,128)S(1)} %get-tuple-element.33) | copy-start | bytes 393220
  22.2 8.1 %copy-start.15 = (f32[2,128,128]{2,1,0:T(8,128)}, f32[2,128,128]{2,1,0:T(8,128)S(1)}, u32[]{:S(2)}) copy-start(f32[2,128,128]{2,1,0:T(8,128)S(1)} %get-tuple-element.34) | copy-start | bytes 393220
  22.2 8.1 %copy-start.16 = (f32[2,128,128]{2,1,0:T(8,128)}, f32[2,128,128]{2,1,0:T(8,128)S(1)}, u32[]{:S(2)}) copy-start(f32[2,128,128]{2,1,0:T(8,128)S(1)} %get-tuple-element.35) | copy-start | bytes 393220
  22.2 8.1 %copy-start.17 = (f32[2,128,128]{2,1,0:T(8,128)}, f32[2,128,128]{2,1,0:T(8,128)S(1)}, u32[]{:S(2)}) copy-start(f32[2,128,128]{2,1,0:T(8,128)S(1)} %get-tuple-element.36) | copy-start | bytes 393220
  22.2 8.1 %copy-start.18 = (f32[2,128,128]{2,1,0:T(8,128)}, f32[2,128,128]{2,1,0:T(8,128)S(1)}, u32[]{:S(2)}) copy-start(f32[2,128,128]{2,1,0:T(8,128)S(1)} %get-tuple-element.37) | copy-start | bytes 393220
  22.2 8.1 %copy-start.19 = (f32[2,128,128]{2,1,0:T(8,128)}, f32[2,128,128]{2,1,0:T(8,128)S(1)}, u32[]{:S(2)}) copy-start(f32[2,128,128]{2,1,0:T(8,128)S(1)} %get-tuple-element.38) | copy-start | bytes 393220
  30.3 11.4 %collective-permute-start.4 = (f32[2,3,1,128,128]{4,3,2,1,0:T(8,128)S(1)}, f32[2,3,1,128,128]{4,3,2,1,0:T(8,128)S(1)}, u32[]{:S(2)}, u32[]{:S(2)}) collective-permute-start(f32[2,3,1,128,128]{4,3,2,1,0:T(8,128)S(1)} %get-tuple-element.12), channel_id=1, source_target_pairs={{0,8},{8,16},{16,24},{24,32},{32,40},{40,48},{48,56},{56,64},{64,7... | collective-permute-start | bytes 1179656 | tf_op jit(solution)/shard_map/ppermute | solution.py:15
  32.3 11.2 %collective-permute-start.5 = (f32[2,3,1,128,128]{4,3,2,1,0:T(8,128)S(1)}, f32[2,3,1,128,128]{4,3,2,1,0:T(8,128)S(1)}, u32[]{:S(2)}, u32[]{:S(2)}) collective-permute-start(f32[2,3,1,128,128]{4,3,2,1,0:T(8,128)S(1)} %get-tuple-element.13), channel_id=1, source_target_pairs={{8,0},{16,8},{24,16},{32,24},{40,32},{48,40},{56,48},{64,56},{72,6... | collective-permute-start | bytes 1179656 | tf_op jit(solution)/shard_map/ppermute | solution.py:17
  50.5 10.0 %copy-start.26 = (f32[16,3,2,16,128]{4,3,2,1,0:T(8,128)S(1)}, f32[16,3,2,16,128]{4,3,2,1,0:T(8,128)}, u32[]{:S(2)}) copy-start(f32[16,3,2,16,128]{4,3,2,1,0:T(8,128)} %param.5) | copy-start | bytes 2359300
  52.0 33.5 %all-to-all-start = ((f32[2,3,2,128,128]{4,1,2,0,3:T(4,128)}), f32[2,3,2,128,128]{4,1,2,0,3:T(4,128)S(1)}, u32[]{:S(2)}, u32[]{:S(2)}) async-start(f32[2,3,2,128,128]{4,1,2,0,3:T(4,128)} %copy.93), calls=%async_computation | async-start | bytes 2097152 | tf_op jit(solution)/shard_map/all_to_all | solution.py:87
  122.5 26.0 %all-to-all-start.3 = ((f32[16,3,2,16,128]{4,3,2,1,0:T(8,128)}), f32[16,3,2,16,128]{4,3,2,1,0:T(8,128)S(1)}, u32[]{:S(2)}, u32[]{:S(2)}) async-start(f32[16,3,2,16,128]{4,3,2,1,0:T(8,128)} %copy.97), calls=%async_computation.3 | async-start | bytes 1572864 | tf_op jit(solution)/shard_map/all_to_all | solution.py:102

commit v2 on v1

v2 whole, which is shorter than its diff:
```python
import math

import jax
import jax.numpy as jnp
from jax import lax
from jax.experimental import pallas as pl
from jax.experimental.pallas import tpu as pltpu
from jax.sharding import Mesh
from jax.sharding import PartitionSpec as P

STRIP = 16
PART = 0.05 / 16.0


def rows_at(ref, lead, start, shift, height):
    first = start + shift
    if first < 0:
        block = pltpu.roll(ref[lead + (pl.ds(0, STRIP), slice(None))], 1, 0)
        row = lax.broadcasted_iota(jnp.int32, block.shape, 0)
        return jnp.where(row == 0, 0.0, block)
    if first + STRIP > height:
        block = pltpu.roll(ref[lead + (pl.ds(height - STRIP, STRIP), slice(None))], STRIP - 1, 0)
        row = lax.broadcasted_iota(jnp.int32, block.shape, 0)
        return jnp.where(row == STRIP - 1, 0.0, block)
    return ref[lead + (pl.ds(first, STRIP), slice(None))]


def across(block):
    breadth = block.shape[1]
    lane = lax.broadcasted_iota(jnp.int32, block.shape, 1)
    left = jnp.where(lane == 0, 0.0, pltpu.roll(block, 1, 1))
    right = jnp.where(lane == breadth - 1, 0.0, pltpu.roll(block, breadth - 1, 1))
    return left + right


def outer_sum(mid, above, below):
    tall = (mid + mid) + (above + below)
    both = tall + mid
    return across(tall) + (both + both)


def full_sum(mid, pair_y, side, side_y):
    near = pair_y + side
    six = 6.0 * mid
    inner = (near + near) + (six + side_y)
    rest = inner + (near - six)
    return across(inner) + (rest + rest)


def combine(diag, off, fields):
    a, b, c = fields
    return (
        diag[0] * a + off[0] * b + off[1] * c,
        off[0] * a + diag[1] * b + off[2] * c,
        off[1] * a + off[2] * b + diag[2] * c,
    )


def partial_kernel(probes_far, modulus_far, tangent_far, down, up, probes, modulus, tangent, prod, sems):
    count = probes.shape[0]
    height = probes.shape[3]
    pairs = ((modulus_far, modulus), (probes_far, probes), (tangent_far, tangent))
    copies = [pltpu.make_async_copy(src, dst, sems.at[n]) for n, (src, dst) in enumerate(pairs)]
    for copy in copies:
        copy.start()
    copies[0].wait()
    copies[1].wait()
    for z in range(2):
        for k in range(count):
            for i in range(3):
                prod[z * 3 * count + 3 * k + i] = probes[k, i, z] * modulus[z]
    copies[2].wait()
    for z, out in ((0, down), (1, up)):
        other = 1 - z
        for s in range(0, height, STRIP):
            here = pl.ds(s, STRIP)

            def mod(plane, shift):
                return rows_at(modulus, (plane,), s, shift, height)

            m = mod(z, 0)
            side = mod(other, 0)
            neighbours = full_sum(m, mod(z, -1) + mod(z, 1), side, mod(other, -1) + mod(other, 1))
            common = (3.4 / 16.0) * m + PART * neighbours - 1.0
            diag = [common + 0.125 * tangent[i, z, here, :] for i in range(3)]
            off = [0.125 * tangent[3 + i, z, here, :] for i in range(3)]
            scaled = PART * m
            out[6 * count, here, :] = m
            for k in range(count):
                values = [probes[k, i, z, here, :] for i in range(3)]
                mixed = combine(diag, off, values)
                for i in range(3):
                    def val(plane, shift):
                        return rows_at(probes, (k, i, plane), s, shift, height)

                    def pro(plane, shift):
                        return rows_at(prod, (plane * 3 * count + 3 * k + i,), s, shift, height)

                    first = full_sum(values[i], val(z, -1) + val(z, 1), val(other, 0), val(other, -1) + val(other, 1))
                    second = full_sum(pro(z, 0), pro(z, -1) + pro(z, 1), pro(other, 0), pro(other, -1) + pro(other, 1))
                    out[3 * k + i, here, :] = values[i]
                    out[3 * count + 3 * k + i, here, :] = mixed[i] - scaled * first - PART * second


def filter_kernel(lo, down, up, hi, tangent, out, once, prod, sums, products, prior):
    planes = (lo, down, up, hi)
    total = (lo.shape[0] - 1) // 2
    count = total // 3
    height = lo.shape[1]
    for z in range(4):
        for n in range(total):
            prior[z * total + n] = planes[z][n] * planes[z][2 * total]
    for source, target in ((0, 1), (1, 0), (2, 3), (3, 2)):
        src = planes[source]
        dst = planes[target]
        for s in range(0, height, STRIP):
            here = pl.ds(s, STRIP)

            def at(ref, n, shift):
                return rows_at(ref, (n,), s, shift, height)

            m = dst[2 * total, here, :]
            weight = PART * outer_sum(at(src, 2 * total, 0), at(src, 2 * total, -1), at(src, 2 * total, 1))
            scaled = PART * m
            for n in range(total):
                first = outer_sum(at(src, n, 0), at(src, n, -1), at(src, n, 1))
                j = source * total + n
                second = outer_sum(at(prior, j, 0), at(prior, j, -1), at(prior, j, 1))
                value = dst[total + n, here, :] + weight * dst[n, here, :] - scaled * first - PART * second
                if target in (0, 3):
                    value = jnp.where(m > 0.0, value, 0.0)
                once[target * total + n, here, :] = value
                prod[target * total + n, here, :] = value * m
    for z in (1, 2):
        for n in range(total):
            sums[(z - 1) * total + n] = once[(z - 1) * total + n] + once[(z + 1) * total + n]
            products[(z - 1) * total + n] = prod[(z - 1) * total + n] + prod[(z + 1) * total + n]
    for z in (1, 2):
        plane = planes[z]
        for s in range(0, height, STRIP):
            here = pl.ds(s, STRIP)

            def at(ref, n, shift):
                return rows_at(ref, (n,), s, shift, height)

            def mod(p, shift):
                return rows_at(planes[p], (2 * total,), s, shift, height)

            m = mod(z, 0)
            side = [mod(z - 1, d) + mod(z + 1, d) for d in (-1, 0, 1)]
            neighbours = full_sum(m, mod(z, -1) + mod(z, 1), side[1], side[0] + side[2])
            common = (6.8 / 16.0) * m + (2.0 * PART) * neighbours - 2.0
            diag = [common + 0.25 * tangent[i, z - 1, here, :] for i in range(3)]
            off = [0.25 * tangent[3 + i, z - 1, here, :] for i in range(3)]
            scaled = (2.0 * PART) * m
            for k in range(count):
                base = z * total + 3 * k
                mixed = combine(diag, off, [once[base + i, here, :] for i in range(3)])
                for i in range(3):
                    n = base + i
                    j = n - total
                    first = full_sum(at(once, n, 0), at(once, n, -1) + at(once, n, 1), at(sums, j, 0), at(sums, j, -1) + at(sums, j, 1))
                    second = full_sum(at(prod, n, 0), at(prod, n, -1) + at(prod, n, 1), at(products, j, 0), at(products, j, -1) + at(products, j, 1))
                    value = mixed[i] - scaled * first - (2.0 * PART) * second - plane[3 * k + i, here, :]
                    out[s // STRIP, k, i, z - 1] = value


VM = pl.BlockSpec(memory_space=pltpu.VMEM)


def partial_call(probes, modulus, tangent, **kw):
    count, _, _, height, breadth = probes.shape
    pack = pltpu.VMEM((6 * count + 1, height, breadth), jnp.float32)
    return pl.pallas_call(
        partial_kernel,
        out_shape=(pack, pack),
        in_specs=[pl.BlockSpec(memory_space=pl.ANY)] * 3,
        out_specs=(VM, VM),
        scratch_shapes=[pltpu.VMEM(a.shape, jnp.float32) for a in (probes, modulus, tangent)]
        + [pltpu.VMEM((6 * count, height, breadth), jnp.float32), pltpu.SemaphoreType.DMA((3,))],
        compiler_params=pltpu.CompilerParams(vmem_limit_bytes=20 << 20),
        name="partial",
        **kw,
    )(probes, modulus, tangent)


def filter_call(lo, down, up, hi, tangent, **kw):
    packed, height, breadth = lo.shape
    total = (packed - 1) // 2
    count = total // 3
    plane = lambda n: pltpu.VMEM((n, height, breadth), jnp.float32)
    return pl.pallas_call(
        filter_kernel,
        out_shape=pltpu.VMEM((height // STRIP, count, 3, 2, STRIP, breadth), jnp.float32),
        in_specs=[VM] * 5,
        out_specs=VM,
        scratch_shapes=[plane(4 * total), plane(4 * total), plane(2 * total), plane(2 * total), plane(4 * total)],
        compiler_params=pltpu.CompilerParams(vmem_limit_bytes=24 << 20),
        name="filter",
        **kw,
    )(*(pltpu.with_memory_space_constraint(a, pltpu.VMEM) for a in (lo, down, up, hi, tangent)))


def sum_over(block, axes, count):
    copies = jnp.broadcast_to(block[None], (count,) + block.shape)
    return jnp.sum(lax.all_to_all(copies, axes, 0, 0, tiled=True), axis=0)


def body(probes, earlier, modulus, tangent, slabs, columns, scale):
    highest = lax.Precision.HIGHEST
    down, up = partial_call(probes, modulus, tangent)
    places = ("x", "y", "core")
    ends = slabs - 1
    lo = lax.ppermute(up, places, [(i, i + 1) for i in range(ends)])
    hi = lax.ppermute(down, places, [(i + 1, i) for i in range(ends)])
    filtered = filter_call(lo, down, up, hi, tangent)
    filtered, earlier = lax.optimization_barrier((filtered, earlier))
    rows_y = lax.all_to_all(filtered, "probe", 0, 0, tiled=True)
    rows_y, earlier = lax.optimization_barrier((rows_y, earlier))
    kept = earlier.shape[0]
    both = jnp.concatenate([earlier, rows_y.reshape(earlier.shape)], axis=0)
    dims = (1, 2, 3, 4)
    gram = lax.dot_general(both, both, ((dims, dims), ((), ())), precision=highest)
    total = gram.shape[0]
    gram = gram.reshape(8, total * total // 8)
    gram = sum_over(gram, ("probe", "core"), 2 * columns)
    gram = sum_over(gram, ("x", "y"), slabs // 2).reshape(total, total)
    factor = jnp.linalg.cholesky(gram)
    inverse = jax.scipy.linalg.solve_triangular(factor, jnp.eye(total, dtype=jnp.float32), lower=True)
    coeff = jnp.dot(inverse[:kept, :kept].T, factor[kept:, :kept].T, precision=highest)
    basis_rows = lax.dot_general(
        inverse[kept:] * scale, both, (((1,), (0,)), ((), ())), precision=highest
    ).reshape(filtered.shape)
    correlation = coeff * scale
    basis_rows, correlation = lax.optimization_barrier((basis_rows, correlation))
    blocks = lax.all_to_all(basis_rows, "probe", 0, 0, tiled=True)
    basis = jnp.transpose(blocks, (1, 2, 3, 0, 4, 5)).reshape(probes.shape)
    return (basis, correlation)


def solution(mesh):
    slabs = mesh.shape["slab"]
    columns = mesh.shape["probe"]
    side = math.isqrt(slabs // 2)
    wide = Mesh(mesh.devices.reshape(side, side, 2, columns), ("x", "y", "core", "probe"))
    slab = ("x", "y", "core")
    in_specs = (
        P("probe", None, slab, None, None),
        P(None, None, slab, "probe", None),
        P(slab, None, None),
        P(None, slab, None, None),
    )
    out_specs = (P("probe", None, slab, None, None), P())

    def step(probes, earlier, modulus, tangent):
        length = math.prod(probes.shape[1:])
        scale = jnp.sqrt(jnp.float32(length))
        inner = lambda *parts: body(*parts, slabs, columns, scale)
        return jax.shard_map(inner, mesh=wide, in_specs=in_specs, out_specs=out_specs, check_vma=False)(
            probes, earlier, modulus, tangent
        )

    return step
```

time: 152 us -> 119 us (0.78); the launches traced: 149 us -> 119 us
  blocking collectives: 25.9 us -> 79.6 us
  waiting for transfers between devices: 50.5 us -> 10.2 us
  starting transfers between devices: 35.2 us -> 7.67 us
  other arithmetic: 25 us -> 6.73 us
  Pallas kernels: 0 us -> 4.83 us
  local copies, waits for them, and re-layouts: 8.27 us -> 5.72 us
    all_to_all x2 -> x4, blocking collectives: 25.9 us -> 79.6 us  [the longest x1 31.4 us: body(): rows_y = lax.all_to_all(filtered, 'probe', 0, 0, tiled=True)]
    all_to_all x2 -> x0, waiting for transfers between devices: 46.2 us -> none  [the longest x1 24.6 us: body(): lax.all_to_all(filtered, 'probe', split_axis=3, concat_axis=0, tiled=True)]
    ppermute x6 -> x2, starting transfers between devices: 23.2 us -> 7.67 us  [the longest x1 5.75 us: body(): hi = lax.ppermute(down, places, [(i + 1, i) for i in range(ends)])]
    all_to_all x2 -> x0, starting transfers between devices: 12 us -> none  [the longest x1 8.47 us: body(): lax.all_to_all(filtered, 'probe', split_axis=3, concat_axis=0, tiled=True)]
    ppermute x6 -> x2, waiting for transfers between devices: 4.32 us -> 10.2 us  [the longest x1 8.43 us: body(): lo = lax.ppermute(up, places, [(i, i + 1) for i in range(ends)])]
    sub x1 -> x0, other arithmetic: 5.5 us -> none  [body(): filtered = 2.0 * second - probes]
    div x1 -> x0, other arithmetic: 5.17 us -> none  [scaled_tangent(): return (summed + local_part - 8.0 * centre) / 8.0]
    pallas_call x0 -> x2, Pallas kernels: none -> 4.83 us  [the longest x1 3.2 us: filter_call(): pl.pallas_call(filter_kernel, out_shape=pltpu.VMEM((height // STRIP, coun...]
  transfers between devices with their start and end apart: 8 -> 2, of which waited for: 5 -> 2; matrix products, arithmetic and copies ran while one was open for 6% -> 0% of each run, Pallas kernels for 0% -> 0%
where the time goes in v2:
time: 119 us
  blocking collectives  79.6 us (67%)
  waiting for transfers between devices  10.2 us (9%)
  starting transfers between devices  7.67 us (6%)
  other arithmetic  6.73 us (6%)
  local copies, waits for them, and re-layouts  5.72 us (5%)
  Pallas kernels  4.83 us (4%)
  matrix products  3.27 us (3%)
    all_to_all x1, blocking collectives, body(): rows_y = lax.all_to_all(filtered, 'probe', 0, 0, tiled=True)  31.4 us
    all_to_all x1, blocking collectives, body(): blocks = lax.all_to_all(basis_rows, 'probe', 0, 0, tiled=True)  24.9 us
    all_to_all x2, blocking collectives, sum_over(): return jnp.sum(lax.all_to_all(copies, axes, 0, 0, tiled=True), axis=0)  23.3 us
    ppermute x1, waiting for transfers between devices, body(): lo = lax.ppermute(up, places, [(i, i + 1) for i in range(ends)])  8.43 us
    ppermute x1, starting transfers between devices, body(): hi = lax.ppermute(down, places, [(i + 1, i) for i in range(ends)])  5.75 us
    unnamed x11, local copies, waits for them, and re-layouts  3.63 us
    another operation x3, other arithmetic, body(): factor = jnp.linalg.cholesky(gram)  3.6 us
    pallas_call x1, Pallas kernels, filter_call(): pl.pallas_call(filter_kernel, out_shape=pltpu.VMEM((height // STRIP, coun...  3.2 us
  transfers between devices with their start and end apart: 2, of which 2 were waited for; matrix products, arithmetic and copies ran while one was open for 0% of the time, Pallas kernels for 0%

profile of v2, /device:TPU:2, one launch (start us, length us, event | category | flops | bytes accessed | tf_op | source)
XLA Modules:
  0.0 118.7 jit_solution(6846642276655185057)
XLA Ops:
  0.6 0.0 copy-start
  0.6 1.1 copy-done
  1.8 0.0 copy-start.2
  1.8 1.1 copy-done.2
  2.9 0.0 copy-start.3
  2.9 0.9 copy-done.3
  3.8 0.0 copy-start.1
  3.8 1.6 %partial.1 = (f32[13,128,128]{2,1,0:T(8,128)S(1)}, f32[13,128,128]{2,1,0:T(8,128)S(1)}) custom-call(f32[2,3,2,128,128]{4,3,2,1,0:T(8,128)S(1)} %copy-done.2, f32[2,128,128]{2,1,0:T(8,128)S(1)} %copy-done.3, f32[6,2,128,128]{3,2,1,0:T(8,128)S(1)} %copy-done), custom_call_target="tpu_custom_call" | custom-call | tf_op jit(solution)/shard_map/partial/pallas_call | solution.py:174
  5.4 1.9 %collective-permute-start = (f32[13,128,128]{2,1,0:T(8,128)S(1)}, f32[13,128,128]{2,1,0:T(8,128)S(1)}, u32[]{:S(2)}, u32[]{:S(2)}) collective-permute-start(f32[13,128,128]{2,1,0:T(8,128)S(1)} %get-tuple-element.10.up), channel_id=1, source_target_pairs={{0,8},{8,16},{16,24},{24,32},{32,40},{40,48},{48,56},{56,64},{64,7... | collective-permute-start | bytes 2555912 | tf_op jit(solution)/shard_map/ppermute | solution.py:214
  7.4 5.8 %collective-permute-start.1 = (f32[13,128,128]{2,1,0:T(8,128)S(1)}, f32[13,128,128]{2,1,0:T(8,128)S(1)}, u32[]{:S(2)}, u32[]{:S(2)}) collective-permute-start(f32[13,128,128]{2,1,0:T(8,128)S(1)} %get-tuple-element.11.down), channel_id=1, source_target_pairs={{8,0},{16,8},{24,16},{32,24},{40,32},{48,40},{56,48},{64,56},{72,6... | collective-permute-start | bytes 2555912 | tf_op jit(solution)/shard_map/ppermute | solution.py:215
  13.1 8.4 %collective-permute-done.lo = f32[13,128,128]{2,1,0:T(8,128)S(1)} collective-permute-done((f32[13,128,128]{2,1,0:T(8,128)S(1)}, f32[13,128,128]{2,1,0:T(8,128)S(1)}, u32[]{:S(2)}, u32[]{:S(2)}) %collective-permute-start) | collective-permute-done | bytes 852000 | tf_op jit(solution)/shard_map/ppermute | solution.py:214
  21.6 1.8 %collective-permute-done.1.hi = f32[13,128,128]{2,1,0:T(8,128)S(1)} collective-permute-done((f32[13,128,128]{2,1,0:T(8,128)S(1)}, f32[13,128,128]{2,1,0:T(8,128)S(1)}, u32[]{:S(2)}, u32[]{:S(2)}) %collective-permute-start.1) | collective-permute-done | bytes 852000 | tf_op jit(solution)/shard_map/ppermute | solution.py:215
  23.3 0.0 copy-done.1
  23.3 3.2 %filter.1 = f32[8,2,3,2,16,128]{5,4,3,2,1,0:T(8,128)S(1)} custom-call(f32[13,128,128]{2,1,0:T(8,128)S(1)} %collective-permute-done.lo, f32[13,128,128]{2,1,0:T(8,128)S(1)} %get-tuple-element.11.down, f32[13,128,128]{2,1,0:T(8,128)S(1)} %get-tuple-element.10.up, f32[13,128,128]{2,1,0:T(8,128)S(1)} %collective-permute-done.1.hi, f32[6,2,128,128]{3,2,1,0:T(8,128)S(1)} %copy-done.1), custom_call_target="tpu_custom_call" | custom-call | tf_op jit(solution)/shard_map/filter/pallas_call | solution.py:192
  26.5 0.0 copy-start.4
  26.5 31.4 %all_to_all.20 = f32[8,2,3,2,16,128]{5,4,3,2,1,0:T(8,128)S(1)} all-to-all(f32[8,2,3,2,16,128]{5,4,3,2,1,0:T(8,128)S(1)} %filter.1), channel_id=1, replica_groups=mesh['x'=4,'y'=4,'core'=2,'probe'=8] {'probe'}, dimensions={0} | all-to-all | bytes 1572864 | tf_op jit(solution)/shard_map/all_to_all | solution.py:218
  58.0 0.0 copy-done.4
  58.0 0.5 copy_dynamic-update-slice_fusion.1
  58.4 0.5 copy_dynamic-update-slice_fusion
  58.9 1.4 %convolution_bitcast_fusion = f32[32,32]{1,0:T(8,128)S(1)} fusion(f32[32,3,2,16,128]{4,0,3,2,1:T(8,128)S(1)} %copy_dynamic-update-slice_fusion), kind=kOutput, calls=%fused_computation | convolution fusion | flops 150994944 | bytes 1576960 | tf_op jit(solution)/shard_map/dot_general | solution.py:223
  60.3 0.1 broadcast_in_dim.7
  60.3 10.4 %all_to_all.21 = f32[16,8,128]{2,1,0:T(8,128)S(1)} all-to-all(f32[16,8,128]{2,1,0:T(8,128)S(1)} %broadcast_in_dim.16), channel_id=1, replica_groups=mesh['x'=4,'y'=4,'core'=2,'probe'=8] {'probe','core'}, dimensions={0} | all-to-all | bytes 131072 | tf_op jit(solution)/shard_map/all_to_all | solution.py:206
  70.8 12.9 %all_to_all.22 = f32[16,8,128]{2,1,0:T(8,128)S(1)} all-to-all(f32[16,8,128]{2,1,0:T(8,128)S(1)} %broadcast_in_dim.17), channel_id=1, replica_groups=mesh['x'=4,'y'=4,'core'=2,'probe'=8] {'x','y'}, dimensions={0} | all-to-all | bytes 131072 | tf_op jit(solution)/shard_map/all_to_all | solution.py:206
  83.7 0.1 reshape.29
  83.7 0.1 copy.26
  83.8 2.9 %cholesky.17 = f32[32,32]{1,0:T(8,128)S(1)} custom-call(f32[32,32]{1,0:T(8,128)S(1)} %fusion.2), custom_call_target="Cholesky" | custom-call | tf_op jit(solution)/shard_map/jit(cholesky)/cholesky | solution.py:228
  86.8 0.6 compare_reduce_fusion
  87.4 0.7 select_bitcast_fusion
  88.1 2.4 %custom-call.7 = f32[1,32,32]{1,2,0:T(8,128)S(1)} custom-call(f32[1,32,32]{2,1,0:T(8,128)S(1)} %get-tuple-element.18), custom_call_target="InvertDiagBlocksLowerTriangular" | custom-call | tf_op jit(solution)/shard_map/jit(_solve_triangular)/triangular_solve | solution.py:229
  90.5 0.2 fusion
  90.7 0.9 fusion.6
  91.6 0.8 convolution_multiply_fusion
  92.4 0.4 copy.27
  92.9 24.9 %all_to_all.23 = f32[8,2,3,2,16,128]{5,1,4,3,2,0:T(2,128)S(1)} all-to-all(f32[8,2,3,2,16,128]{5,1,4,3,2,0:T(2,128)S(1)} %copy.27), channel_id=1, replica_groups=mesh['x'=4,'y'=4,'core'=2,'probe'=8] {'probe'}, dimensions={0} | all-to-all | bytes 1572864 | tf_op jit(solution)/shard_map/all_to_all | solution.py:236
  117.8 1.0 copy.28
  (6 shorter events, 0.1 us)
Async XLA Ops:
  0.6 1.1 copy-start
  1.8 1.1 copy-start.2
  2.9 0.9 copy-start.3
  3.8 19.5 %copy-start.1 = (f32[6,2,128,128]{3,2,1,0:T(8,128)S(1)}, f32[6,2,128,128]{3,2,1,0:T(8,128)}, u32[]{:S(2)}) copy-start(f32[6,2,128,128]{3,2,1,0:T(8,128)} %tangent.1) | copy-start | bytes 2359300
  5.4 16.1 %collective-permute-start = (f32[13,128,128]{2,1,0:T(8,128)S(1)}, f32[13,128,128]{2,1,0:T(8,128)S(1)}, u32[]{:S(2)}, u32[]{:S(2)}) collective-permute-start(f32[13,128,128]{2,1,0:T(8,128)S(1)} %get-tuple-element.10.up), channel_id=1, source_target_pairs={{0,8},{8,16},{16,24},{24,32},{32,40},{40,48},{48,56},{56,64},{64,7... | collective-permute-start | bytes 2555912 | tf_op jit(solution)/shard_map/ppermute | solution.py:214
  7.4 15.9 %collective-permute-start.1 = (f32[13,128,128]{2,1,0:T(8,128)S(1)}, f32[13,128,128]{2,1,0:T(8,128)S(1)}, u32[]{:S(2)}, u32[]{:S(2)}) collective-permute-start(f32[13,128,128]{2,1,0:T(8,128)S(1)} %get-tuple-element.11.down), channel_id=1, source_target_pairs={{8,0},{16,8},{24,16},{32,24},{40,32},{48,40},{56,48},{64,56},{72,6... | collective-permute-start | bytes 2555912 | tf_op jit(solution)/shard_map/ppermute | solution.py:215
  26.5 31.4 %copy-start.4 = (f32[16,3,2,16,128]{4,3,2,1,0:T(8,128)S(1)}, f32[16,3,2,16,128]{4,3,2,1,0:T(8,128)}, u32[]{:S(2)}) copy-start(f32[16,3,2,16,128]{4,3,2,1,0:T(8,128)} %param.6) | copy-start | bytes 2359300
